TPU v7x, 512 devices: a whole 4x8x8 slice. The times are simulated.
512 devices in a mesh: seq: 32 (over x, y), chan: 8 (over z), dp: 2 (over core).
Axes of the slice: x: 4, y: 8, z: 8, core: 2. Of those that a mesh axis runs over, the one named last changes fastest.
Arguments:
- ssm_input: bfloat16 [2, 4096, 4096], P('dp', 'seq', 'chan'), may hold values from -6 to 6
- gate_z: bfloat16 [2, 4096, 4096], P('dp', 'seq', 'chan'), may hold values from -6 to 6
- b_proj: bfloat16 [2, 4096, 128], P('dp', 'seq'), may hold values from -0.52734375 to 0.52734375
- c_proj: bfloat16 [2, 4096, 128], P('dp', 'seq'), may hold values from -6 to 6
- step_size: float32 [2, 4096, 64], P('dp', 'seq', 'chan'), may hold values from 0.02 to 0.2
- log_decay: float32 [2, 4096, 64], P('dp', 'seq', 'chan'), may hold values from -1 to 0, as said below
- skip_d: float32 [64], P('chan'), may hold values from 0.5 to 1.5
- norm_gain: float32 [4096], P('chan'), may hold values from 0.5 to 1.5
- w_out: bfloat16 [4096, 2048], P('chan'), may hold values from -0.09375 to 0.09375
- d_out: bfloat16 [2, 4096, 2048], P('dp', 'seq', 'chan'), may hold values from -6 to 6
- game_lengths: int32 [2, 4], P('dp'), may hold values from 1 to 2048, 4096 in all within a row
Outputs:
- out: bfloat16 [2, 4096, 2048], P('dp', 'seq', 'chan')
- grad_x: bfloat16 [2, 4096, 4096], P('dp', 'seq', 'chan')
- grad_gain: float32 [4096], P('chan')
- grad_skip: float32 [64], P('chan')
Inputs may be any that keep to these rules, and one draw needn't show every extreme that they name: `game_lengths`: each row's 4 game lengths sum to 4096, and the longest is exactly 2048. `log_decay`: a log decay per position and head.
All inputs are finite; a program needn't handle non-finite values.
Results may differ from a plain program's by a relative error of at most 0.017.
Values may be sent and summed in bfloat16 or wider, within the bound.
A program may use at most 64 MiB of HBM per device.

v0:
```python
import jax
import jax.numpy as jnp
from jax import lax
from jax.sharding import Mesh
from jax.sharding import PartitionSpec as P

SEQ = ("seq_0", "seq_1")
SEQ_DP = ("seq_0", "seq_1", "dp")
NORM_EPS = 1e-05


def filled_with(value, identity):
    return jax.tree.map(
        lambda part, zero: jnp.zeros_like(part) + jnp.asarray(zero, part.dtype), value, identity
    )


def prefix_by_axis(value, axes, combine, identity, reverse):
    before = start = filled_with(value, identity)
    so_far = value
    for axis in reversed(axes):
        length, mine = (lax.axis_size(axis), lax.axis_index(axis))
        pieces = jax.tree.map(
            lambda part, kind: lax.all_gather(part.astype(kind), axis),
            so_far,
            (jnp.bfloat16, jnp.bfloat16),
        )
        inside, so_far = (start, start)
        for k in reversed(range(length)) if reverse else range(length):
            passed = k > mine if reverse else k < mine
            so_far = combine(
                so_far, jax.tree.map(lambda part, own: part[k].astype(own.dtype), pieces, value)
            )
            inside = jax.tree.map(lambda new, old: jnp.where(passed, new, old), so_far, inside)
        before = combine(inside, before)
    return before


def in_blocks(value, dim, length):
    lengths = value.shape
    pieces = value.reshape(*lengths[:dim], length, lengths[dim] // length, *lengths[dim + 1 :])
    return jnp.moveaxis(pieces, dim, 0)


def sent_and_summed(value, axis, dim):
    length = lax.axis_size(axis)
    pieces = lax.all_to_all(in_blocks(value, dim, length), axis, 0, 0, tiled=True)
    return jnp.sum(pieces.astype(jnp.float32), axis=0)


def copy_for_each(value, axis):
    length = lax.axis_size(axis)
    return lax.all_to_all(
        jnp.broadcast_to(value[None], (length, *value.shape)), axis, 0, 0, tiled=True
    )


def taken_together(value, axis):
    return copy_for_each(value, axis).sum(axis=0)


def block_parts(c_block, b_block, dt_block, decay_block, reset_block):
    block_len = c_block.shape[0]
    running = jnp.cumsum(decay_block, axis=0)
    reset_count = jnp.cumsum(reset_block, axis=0)
    scores = lax.dot_general(
        c_block, b_block, (((1,), (1,)), ((), ())), preferred_element_type=jnp.float32
    )
    indices = jnp.arange(block_len, dtype=jnp.int32)
    allowed = (indices[:, None] >= indices[None, :]) & (
        reset_count[:, None] == reset_count[None, :]
    )
    log_gap = running.T[:, :, None] - running.T[:, None, :]
    mixing = (
        jnp.where(allowed[None], jnp.exp(jnp.minimum(log_gap, 0.0)), 0.0)
        * scores[None]
        * dt_block.T[:, None, :]
    )
    mixing = mixing.astype(jnp.bfloat16)
    end_count = reset_count[-1]
    carry_weight = jnp.where((reset_count == 0)[:, None], jnp.exp(running), 0.0)
    tail_weight = jnp.where(
        (reset_count == end_count)[:, None], jnp.exp(running[-1][None, :] - running), 0.0
    )
    block_decay = jnp.where(end_count == 0, jnp.exp(running[-1]), 0.0)
    return (mixing, carry_weight, tail_weight, block_decay)


def chain_link(earlier, later):
    return (earlier[0] * later[0], later[0][:, None, None] * earlier[1] + later[1])


def local(
    ssm_input,
    gate_z,
    b_proj,
    c_proj,
    step_size,
    log_decay,
    skip_d,
    norm_gain,
    w_out,
    d_out,
    game_lengths,
):
    seq_len = ssm_input.shape[1]
    local_width = ssm_input.shape[2]
    heads_here = step_size.shape[2]
    head_dim = local_width // heads_here
    state_dim = b_proj.shape[2]
    block_len = min(512, seq_len)
    count_blocks = seq_len // block_len
    total_width = local_width * lax.axis_size("chan")
    x_heads = ssm_input[0].reshape(seq_len, heads_here, head_dim)
    c_rows = c_proj[0]
    b_rows = b_proj[0]
    dt_rows = step_size[0]
    lengths = game_lengths[0]
    starts = jnp.cumsum(lengths) - lengths
    sequence_positions = lax.axis_index(SEQ) * seq_len + jnp.arange(seq_len, dtype=jnp.int32)
    resets = jnp.any(sequence_positions[:, None] == starts[None, :], axis=1).astype(jnp.int32)

    def blocked(array):
        return array.reshape((count_blocks, block_len) + array.shape[1:])

    zero_state = jnp.zeros((heads_here, state_dim, head_dim), jnp.float32)
    unit_decay = jnp.ones((heads_here,), jnp.float32)

    def forward_step(state_pair, block_inputs):
        local_state, before = state_pair
        x_block, c_block, b_block, dt_block, decay_block, reset_block = block_inputs
        mixing, carry_weight, tail_weight, block_decay = block_parts(
            c_block, b_block, dt_block, decay_block, reset_block
        )
        inside = jnp.einsum("hts,shp->thp", mixing, x_block, preferred_element_type=jnp.float32)
        carried = carry_weight[:, :, None] * jnp.einsum(
            "tn,hnp->thp", c_block.astype(jnp.float32), local_state
        )
        scaled = ((tail_weight * dt_block)[:, :, None] * x_block).astype(jnp.bfloat16)
        fresh_state = jnp.einsum("sn,shp->hnp", b_block, scaled, preferred_element_type=jnp.float32)
        new_pair = (block_decay[:, None, None] * local_state + fresh_state, before * block_decay)
        return (
            new_pair,
            (
                inside + carried,
                carry_weight * before[None, :],
                mixing,
                carry_weight,
                tail_weight,
                block_decay,
            ),
        )

    forward_inputs = (
        blocked(x_heads),
        blocked(c_rows),
        blocked(b_rows),
        blocked(dt_rows),
        blocked(log_decay[0]),
        blocked(resets),
    )
    (dev_state, dev_decay), (
        ssd_blocks,
        incoming_weight,
        mixings,
        carry_weights,
        tail_weights,
        block_decays,
    ) = lax.scan(forward_step, (zero_state, unit_decay), forward_inputs)
    _, incoming = prefix_by_axis(
        (dev_decay, dev_state), SEQ, chain_link, (unit_decay, zero_state), False
    )
    from_left = jnp.einsum("tn,hnp->thp", c_rows.astype(jnp.float32), incoming)
    ssd_out = (
        ssd_blocks.reshape(seq_len, heads_here, head_dim)
        + incoming_weight.reshape(seq_len, heads_here)[:, :, None] * from_left
    )
    ssd_out = ssd_out + skip_d[None, :, None] * x_heads.astype(jnp.float32)
    gate_act = jax.nn.silu(gate_z[0].astype(jnp.float32))
    gated = ssd_out.reshape(seq_len, local_width) * gate_act
    square_total = lax.psum(jnp.sum(gated * gated, axis=1), "chan")
    inv_rms = lax.rsqrt(square_total / total_width + NORM_EPS)
    normed = (gated * norm_gain).astype(jnp.bfloat16)
    w_cols = w_out
    projected = sent_and_summed(
        lax.dot_general(
            w_cols, normed, (((0,), (1,)), ((), ())), preferred_element_type=jnp.float32
        ).astype(jnp.bfloat16),
        "chan",
        0,
    ).T
    out = (inv_rms[:, None] * projected).astype(jnp.bfloat16)[None]
    cotangent = d_out[0]
    w_cols = w_out
    pulled = lax.dot_general(
        lax.all_gather(cotangent, "chan", axis=1, tiled=True),
        w_cols,
        (((1,), (1,)), ((), ())),
        preferred_element_type=jnp.float32,
    )
    out_dot = lax.psum(jnp.sum(cotangent.astype(jnp.float32) * projected, axis=1), "chan")
    d_normed = inv_rms[:, None] * pulled
    gain_local = jnp.sum(gated * d_normed, axis=0)
    d_ssd = (
        (norm_gain * d_normed - (inv_rms**3 * out_dot / total_width)[:, None] * gated) * gate_act
    ).astype(jnp.bfloat16)
    d_heads = d_ssd.reshape(seq_len, heads_here, head_dim)
    skip_local = jnp.sum(d_heads.astype(jnp.float32) * x_heads.astype(jnp.float32), axis=(0, 2))
    grad_gain, grad_skip = (taken_together(gain_local, SEQ_DP), taken_together(skip_local, SEQ_DP))

    def backward_step(state_pair, block_inputs):
        local_adjoint, later_decay = state_pair
        d_block, c_block, b_block, dt_block, mixing, carry_weight, tail_weight, block_decay = (
            block_inputs
        )
        inside = jnp.einsum("hts,thp->shp", mixing, d_block, preferred_element_type=jnp.float32)
        carried = (dt_block * tail_weight)[:, :, None] * jnp.einsum(
            "sn,hnp->shp", b_block.astype(jnp.float32), local_adjoint
        )
        weighted = (carry_weight[:, :, None] * d_block).astype(jnp.bfloat16)
        fresh_adjoint = jnp.einsum(
            "tn,thp->hnp", c_block, weighted, preferred_element_type=jnp.float32
        )
        new_pair = (
            fresh_adjoint + block_decay[:, None, None] * local_adjoint,
            later_decay * block_decay,
        )
        return (new_pair, (inside + carried, dt_block * tail_weight * later_decay[None, :]))

    backward_inputs = (
        blocked(d_heads),
        blocked(c_rows),
        blocked(b_rows),
        blocked(dt_rows),
        mixings,
        carry_weights,
        tail_weights,
        block_decays,
    )
    (dev_adjoint, _), (grad_blocks, outgoing_weight) = lax.scan(
        backward_step, (zero_state, unit_decay), backward_inputs, reverse=True
    )
    _, from_right = prefix_by_axis(
        (dev_decay, dev_adjoint), SEQ, chain_link, (unit_decay, zero_state), True
    )
    right_terms = jnp.einsum("sn,hnp->shp", b_rows.astype(jnp.float32), from_right)
    grad_heads = (
        grad_blocks.reshape(seq_len, heads_here, head_dim)
        + outgoing_weight.reshape(seq_len, heads_here)[:, :, None] * right_terms
    )
    grad_heads = grad_heads + skip_d[None, :, None] * d_heads.astype(jnp.float32)
    grad_x = grad_heads.astype(jnp.bfloat16).reshape(1, seq_len, local_width)
    return (out, grad_x, grad_gain, grad_skip)


def solution(mesh):
    finer = Mesh(
        mesh.devices.reshape(4, 8, mesh.shape["chan"], mesh.shape["dp"]),
        ("seq_0", "seq_1", "chan", "dp"),
    )
    return jax.shard_map(
        local,
        mesh=finer,
        in_specs=(
            P("dp", SEQ, "chan"),
            P("dp", SEQ, "chan"),
            P("dp", SEQ, None),
            P("dp", SEQ, None),
            P("dp", SEQ, "chan"),
            P("dp", SEQ, "chan"),
            P("chan"),
            P("chan"),
            P("chan", None),
            P("dp", SEQ, "chan"),
            P("dp", None),
        ),
        out_specs=(P("dp", SEQ, "chan"), P("dp", SEQ, "chan"), P("chan"), P("chan")),
        check_vma=False,
    )
```

profile of v0, /device:TPU:8, one launch (start us, length us, event | category | flops | bytes accessed | tf_op | source)
XLA Modules:
  0.0 205.9 jit_solution(17596666255649511182)
XLA Ops:
  7.2 0.0 all-gather.9.cloned.1.call-start
  7.3 1.0 reduce-window_clone.1
  8.3 0.7 subtract_bitcast_fusion
  8.9 0.1 compare_reduce_fusion
  9.0 0.1 copy.85
  9.1 0.2 broadcast_in_dim.163
  9.3 0.5 slice.212
  9.8 0.1 reduce.5
  10.6 0.8 copy.86
  11.4 0.2 reduce_window_sum.27
  11.6 0.7 broadcast_compare_fusion.1
  12.2 0.8 copy.89
  13.0 0.1 exponential_select_fusion
  13.2 0.1 copy.94
  13.4 0.9 fusion.16
  14.3 0.1 copy.95
  14.4 0.8 fusion.14
  15.3 19.1 %all-gather.3 = bf16[8,1,8]{2,1,0:T(2,128)(2,1)S(1)} all-gather(bf16[1,1,8]{2,1,0:T(2,128)(2,1)S(1)} %get-tuple-element.116), channel_id=1, replica_groups=mesh['seq_0'=4,'seq_1'=8,'chan'=8,'dp'=2] {'seq_1'}, dimensions={0}, use_global_device_ids=true | all-gather | bytes 144 | tf_op jit(solution)/shard_map/all_gather | solution.py:24
  34.4 0.5 convert_bitcast_fusion.2
  34.9 7.0 %all-gather.4 = bf16[4,1,8]{2,1,0:T(2,128)(2,1)S(1)} all-gather(bf16[1,1,8]{2,1,0:T(2,128)(2,1)S(1)} %get-tuple-element.121), channel_id=1, replica_groups=mesh['seq_0'=4,'seq_1'=8,'chan'=8,'dp'=2] {'seq_0'}, dimensions={0}, use_global_device_ids=true | all-gather | bytes 80 | tf_op jit(solution)/shard_map/all_gather | solution.py:24
  41.9 0.1 copy.91
  42.0 0.1 copy.87
  42.1 0.1 copy.96
  42.3 0.5 broadcast_select_fusion.7
  42.8 0.5 fusion.179
  43.4 0.1 fusion.147
  43.5 0.1 fusion.154
  43.6 0.2 fusion.9
  43.8 16.6 %all-gather.9.cloned.1.call-done = bf16[64,128,64]{1,2,0:T(8,128)(2,1)} async-done(((bf16[8,128,64]{1,2,0:T(8,128)(2,1)}), bf16[64,128,64]{1,2,0:T(8,128)(2,1)}) %all-gather.9.cloned.1.call-update) | async-done | bytes 1048592 | tf_op jit(solution)/shard_map/all_gather | solution.py:24
  60.5 1.6 fusion.79
  62.1 13.1 %all_gather.41 = bf16[4,8,128,64]{2,3,1,0:T(8,128)(2,1)S(1)} all-gather(bf16[1,8,128,64]{2,3,1,0:T(8,128)(2,1)S(1)} %fusion.79), channel_id=1, replica_groups=mesh['seq_0'=4,'seq_1'=8,'chan'=8,'dp'=2] {'seq_0'}, dimensions={0}, use_global_device_ids=true | all-gather | bytes 655360 | tf_op jit(solution)/shard_map/all_gather | solution.py:24
  75.2 1.9 fusion.8
  77.2 0.9 multiply_reduce_fusion.1
  78.1 0.8 copy.97
  79.0 1.4 convolution_convert_fusion
  80.4 0.8 copy.110
  81.2 7.6 %all-to-all-start = ((bf16[8,256,128]{1,2,0:T(8,128)(2,1)}), bf16[8,256,128]{1,2,0:T(8,128)(2,1)S(1)}, u32[]{:S(2)}, u32[]{:S(2)}) async-start(bf16[8,256,128]{1,2,0:T(8,128)(2,1)} %bitcast.430), calls=%async_computation | async-start | bytes 1048576 | tf_op jit(solution)/shard_map/all_to_all | solution.py:47
  88.9 0.1 copy.100
  89.0 29.6 %all-gather.1 = bf16[1,128,2048]{2,1,0:T(8,128)(2,1)S(1)} all-gather(bf16[1,128,256]{2,1,0:T(8,128)(2,1)S(1)} %copy-done.6), channel_id=3, replica_groups=mesh['seq_0'=4,'seq_1'=8,'chan'=8,'dp'=2] {'chan'}, dimensions={2}, use_global_device_ids=true | all-gather | bytes 589824 | tf_op jit(solution)/shard_map/all_gather | solution.py:196
  118.6 0.1 convert_reduce_fusion
  118.7 0.9 fusion.88
  119.7 16.8 %all-reduce = (f32[128]{0:T(128)S(1)}, f32[128]{0:T(128)S(1)}) all-reduce(f32[128]{0:T(128)} %get-tuple-element.140, f32[128]{0:T(128)S(1)} %fusion.88), channel_id=1, replica_groups=mesh['seq_0'=4,'seq_1'=8,'chan'=8,'dp'=2] {'chan'}, use_global_device_ids=true, to_apply=%region_5.6 | all-reduce | flops 256 | bytes 2048 | tf_op jit(solution)/shard_map/psum | solution.py:181
  136.6 2.0 fusion.18
  138.7 0.1 copy.101
  138.8 0.8 fusion.13
  139.7 9.3 %all-gather.5 = bf16[4,1,8]{2,1,0:T(2,128)(2,1)S(1)} all-gather(bf16[1,1,8]{2,1,0:T(2,128)(2,1)S(1)} %copy-done.28), channel_id=1, replica_groups=mesh['seq_0'=4,'seq_1'=8,'chan'=8,'dp'=2] {'seq_0'}, dimensions={0}, use_global_device_ids=true | all-gather | bytes 80 | tf_op jit(solution)/shard_map/all_gather | solution.py:24
  149.0 0.2 fusion.7
  149.2 0.1 reduce_sum.76
  149.3 0.1 reduce_sum.77
  149.4 0.6 broadcast_in_dim.174
  150.0 6.1 %all-to-all-start.2 = ((f32[64,1,8]{2,1,0:T(1,128)}), f32[64,1,8]{2,1,0:T(1,128)S(1)}, u32[]{:S(2)}, u32[]{:S(2)}) async-start(f32[64,1,8]{2,1,0:T(1,128)} %broadcast_in_dim.174), calls=%async_computation.2 | async-start | bytes 65536 | tf_op jit(solution)/shard_map/all_to_all | solution.py:53
  156.1 8.5 %all-to-all-done.2 = f32[64,1,8]{2,1,0:T(1,128)S(1)} async-done(((f32[64,1,8]{2,1,0:T(1,128)}), f32[64,1,8]{2,1,0:T(1,128)S(1)}, u32[]{:S(2)}, u32[]{:S(2)}) %all-to-all-start.2) | async-done | bytes 2080 | tf_op jit(solution)/shard_map/all_to_all | solution.py:53
  164.6 0.7 broadcast_in_dim.173
  165.3 5.4 %all-to-all-start.1 = ((f32[64,1,512]{2,1,0:T(1,128)}), f32[64,1,512]{2,1,0:T(1,128)S(1)}, u32[]{:S(2)}, u32[]{:S(2)}) async-start(f32[64,1,512]{2,1,0:T(1,128)} %broadcast_in_dim.173), calls=%async_computation.1 | async-start | bytes 262144 | tf_op jit(solution)/shard_map/all_to_all | solution.py:53
  170.8 0.1 copy.99
  170.9 0.7 fusion.145
  171.6 0.6 reduce_sum.78
  172.2 8.5 %all-to-all-done.1 = f32[64,1,512]{2,1,0:T(1,128)S(1)} async-done(((f32[64,1,512]{2,1,0:T(1,128)}), f32[64,1,512]{2,1,0:T(1,128)S(1)}, u32[]{:S(2)}, u32[]{:S(2)}) %all-to-all-start.1) | async-done | bytes 131104 | tf_op jit(solution)/shard_map/all_to_all | solution.py:53
  180.7 0.7 reduce_sum.74
  181.5 1.6 fusion.62
  183.1 12.8 %all_gather.46 = bf16[4,8,128,64]{2,3,1,0:T(8,128)(2,1)S(1)} all-gather(bf16[1,8,128,64]{2,3,1,0:T(8,128)(2,1)S(1)} %fusion.62), channel_id=1, replica_groups=mesh['seq_0'=4,'seq_1'=8,'chan'=8,'dp'=2] {'seq_0'}, dimensions={0}, use_global_device_ids=true | all-gather | bytes 655360 | tf_op jit(solution)/shard_map/all_gather | solution.py:24
  195.9 1.9 fusion.6
  197.9 0.4 fusion.12
  198.3 0.8 copy.104
  (86 shorter events, 0.5 us)
Async XLA Ops:
  7.2 71.8 %copy-start = (bf16[512,2048]{1,0:T(8,128)(2,1)S(1)}, bf16[512,2048]{1,0:T(8,128)(2,1)}, u32[]{:S(2)}) copy-start(bf16[512,2048]{1,0:T(8,128)(2,1)} %param.19) | copy-start | bytes 6291460
  7.2 34.7 %copy-start.1 = (bf16[1,128,512]{2,1,0:T(8,128)(2,1)S(1)}, bf16[1,128,512]{2,1,0:T(8,128)(2,1)}, u32[]{:S(2)}) copy-start(bf16[1,128,512]{2,1,0:T(8,128)(2,1)} %param.11) | copy-start | bytes 393220
  7.2 7.2 %copy-start.4 = (bf16[1,128,128]{2,1,0:T(8,128)(2,1)S(1)}, bf16[1,128,128]{2,1,0:T(8,128)(2,1)}, u32[]{:S(2)}) copy-start(bf16[1,128,128]{2,1,0:T(8,128)(2,1)} %param.13) | copy-start | bytes 98308
  7.2 34.9 %copy-start.7 = (bf16[1,128,512]{2,1,0:T(8,128)(2,1)S(1)}, bf16[1,128,512]{2,1,0:T(8,128)(2,1)}, u32[]{:S(2)}) copy-start(bf16[1,128,512]{2,1,0:T(8,128)(2,1)} %param.12) | copy-start | bytes 393220
  7.2 36.3 %copy-start.2 = (bf16[1,128,128]{2,1,0:T(8,128)(2,1)S(1)}, bf16[1,128,128]{2,1,0:T(8,128)(2,1)}, u32[]{:S(2)}) copy-start(bf16[1,128,128]{2,1,0:T(8,128)(2,1)} %param.14) | copy-start | bytes 98308
  7.2 53.2 %all-gather.9.cloned.1.call-start = ((), (), s32[]{:S(2)}) async-start(), calls=%async_computation.3 | async-start | bytes 1179648 | tf_op jit(solution)/shard_map/all_gather | solution.py:24
  11.6 30.3 %copy-start.24 = (f32[8]{0:T(128)}, f32[8]{0:T(128)S(1)}, u32[]{:S(2)}) copy-start(f32[8]{0:T(128)S(1)} %fusion.160) | copy-start | bytes 100
  42.1 35.1 %copy-start.22 = (f32[8,128]{1,0:T(8,128)}, f32[8,128]{1,0:T(8,128)S(1)}, u32[]{:S(2)}) copy-start(f32[8,128]{1,0:T(8,128)S(1)} %copy.87) | copy-start | bytes 12292
  43.4 33.8 %copy-start.12 = (f32[8]{0:T(128)}, f32[8]{0:T(128)S(1)}, u32[]{:S(2)}) copy-start(f32[8]{0:T(128)S(1)} %get-tuple-element.125) | copy-start | bytes 100
  43.4 33.8 %copy-start.14 = (f32[8]{0:T(128)}, f32[8]{0:T(128)S(1)}, u32[]{:S(2)}) copy-start(f32[8]{0:T(128)S(1)} %get-tuple-element.126) | copy-start | bytes 100
  43.4 33.8 %copy-start.16 = (f32[8]{0:T(128)}, f32[8]{0:T(128)S(1)}, u32[]{:S(2)}) copy-start(f32[8]{0:T(128)S(1)} %get-tuple-element.127) | copy-start | bytes 100
  43.4 33.8 %copy-start.18 = (f32[8]{0:T(128)}, f32[8]{0:T(128)S(1)}, u32[]{:S(2)}) copy-start(f32[8]{0:T(128)S(1)} %get-tuple-element.128) | copy-start | bytes 100
  43.5 33.7 %copy-start.10 = (pred[128,128]{1,0:T(8,128)(4,1)}, pred[128,128]{1,0:T(8,128)(4,1)S(1)}, u32[]{:S(2)}) copy-start(pred[128,128]{1,0:T(8,128)(4,1)S(1)} %fusion.147) | copy-start | bytes 49156
  43.6 33.6 %copy-start.8 = (f32[128,128]{1,0:T(8,128)}, f32[128,128]{1,0:T(8,128)S(1)}, u32[]{:S(2)}) copy-start(f32[128,128]{1,0:T(8,128)S(1)} %fusion.154) | copy-start | bytes 196612
  75.2 2.0 copy-start.20
  75.2 2.0 copy-start.31
  77.2 1.8 copy-start.30
  80.4 8.6 %copy-start.6 = (bf16[1,128,256]{2,1,0:T(8,128)(2,1)S(1)}, bf16[1,128,256]{2,1,0:T(8,128)(2,1)}, u32[]{:S(2)}) copy-start(bf16[1,128,256]{2,1,0:T(8,128)(2,1)} %param.20) | copy-start | bytes 196612
  81.2 37.4 %all-to-all-start = ((bf16[8,256,128]{1,2,0:T(8,128)(2,1)}), bf16[8,256,128]{1,2,0:T(8,128)(2,1)S(1)}, u32[]{:S(2)}, u32[]{:S(2)}) async-start(bf16[8,256,128]{1,2,0:T(8,128)(2,1)} %bitcast.430), calls=%async_computation | async-start | bytes 1048576 | tf_op jit(solution)/shard_map/all_to_all | solution.py:47
  88.8 92.6 %all-gather.11.cloned.1.call-start = ((), (), s32[]{:S(2)}) async-start(), calls=%async_computation.4 | async-start | bytes 1179648 | tf_op jit(solution)/shard_map/all_gather | solution.py:24
  136.5 2.3 %copy-start.3 = (bf16[1,128,128]{2,1,0:T(8,128)(2,1)S(1)}, bf16[1,128,128]{2,1,0:T(8,128)(2,1)}, u32[]{:S(2)}) copy-start(bf16[1,128,128]{2,1,0:T(8,128)(2,1)} %param.14) | copy-start | bytes 98308
  136.5 2.3 %copy-start.25 = (f32[8]{0:T(128)S(1)}, f32[8]{0:T(128)}, u32[]{:S(2)}) copy-start(f32[8]{0:T(128)} %copy-done.24) | copy-start | bytes 100
  136.5 3.1 %copy-start.28 = (bf16[1,1,8]{2,1,0:T(2,128)(2,1)S(1)}, bf16[1,1,8]{2,1,0:T(2,128)(2,1)}, u32[]{:S(2)}) copy-start(bf16[1,1,8]{2,1,0:T(2,128)(2,1)} %get-tuple-element.120) | copy-start | bytes 52
  136.5 12.5 %copy-start.5 = (bf16[1,128,128]{2,1,0:T(8,128)(2,1)S(1)}, bf16[1,128,128]{2,1,0:T(8,128)(2,1)}, u32[]{:S(2)}) copy-start(bf16[1,128,128]{2,1,0:T(8,128)(2,1)} %param.13) | copy-start | bytes 98308
  138.5 42.9 %copy-start.13 = (f32[8]{0:T(128)S(1)}, f32[8]{0:T(128)}, u32[]{:S(2)}) copy-start(f32[8]{0:T(128)} %copy-done.12) | copy-start | bytes 100
  138.6 42.9 %copy-start.15 = (f32[8]{0:T(128)S(1)}, f32[8]{0:T(128)}, u32[]{:S(2)}) copy-start(f32[8]{0:T(128)} %copy-done.14) | copy-start | bytes 100
  138.6 42.9 %copy-start.17 = (f32[8]{0:T(128)S(1)}, f32[8]{0:T(128)}, u32[]{:S(2)}) copy-start(f32[8]{0:T(128)} %copy-done.16) | copy-start | bytes 100
  138.6 42.9 %copy-start.19 = (f32[8]{0:T(128)S(1)}, f32[8]{0:T(128)}, u32[]{:S(2)}) copy-start(f32[8]{0:T(128)} %copy-done.18) | copy-start | bytes 100
  138.6 42.9 %copy-start.26 = (f32[8]{0:T(128)S(1)}, f32[8]{0:T(128)}, u32[]{:S(2)}) copy-start(f32[8]{0:T(128)} %get-tuple-element.119) | copy-start | bytes 100
  138.6 42.9 %copy-start.27 = (f32[8]{0:T(128)S(1)}, f32[8]{0:T(128)}, u32[]{:S(2)}) copy-start(f32[8]{0:T(128)} %get-tuple-element.122) | copy-start | bytes 100
  138.6 57.3 %copy-start.29 = (f32[8]{0:T(128)S(1)}, f32[8]{0:T(128)}, u32[]{:S(2)}) copy-start(f32[8]{0:T(128)} %get-tuple-element.117) | copy-start | bytes 100
  150.0 14.6 %all-to-all-start.2 = ((f32[64,1,8]{2,1,0:T(1,128)}), f32[64,1,8]{2,1,0:T(1,128)S(1)}, u32[]{:S(2)}, u32[]{:S(2)}) async-start(f32[64,1,8]{2,1,0:T(1,128)} %broadcast_in_dim.174), calls=%async_computation.2 | async-start | bytes 65536 | tf_op jit(solution)/shard_map/all_to_all | solution.py:53
  165.3 15.4 %all-to-all-start.1 = ((f32[64,1,512]{2,1,0:T(1,128)}), f32[64,1,512]{2,1,0:T(1,128)S(1)}, u32[]{:S(2)}, u32[]{:S(2)}) async-start(f32[64,1,512]{2,1,0:T(1,128)} %broadcast_in_dim.173), calls=%async_computation.1 | async-start | bytes 262144 | tf_op jit(solution)/shard_map/all_to_all | solution.py:53
  195.9 2.0 copy-start.9
  195.9 2.0 copy-start.11
  195.9 2.0 copy-start.21
  195.9 2.0 copy-start.23
  195.9 2.0 copy-start.32
Sparse Core Ops, SparseCore 0:
  15.4 45.0 all-gather.8
  139.8 38.7 all-gather.10
where the time goes:
time: 207 us; the launch traced here: 206 us
  blocking collectives  108 us (52%)
  waiting for transfers between devices  33.7 us (16%)
  starting transfers between devices  19.1 us (9%)
  between operations  15.3 us (7%)
  other arithmetic  12 us (6%)
  matrix products  10.7 us (5%)
  local copies, waits for them, and re-layouts  7.31 us (4%)
    all_gather x5, blocking collectives, prefix_by_axis(): lax.all_gather(part.astype(kind), axis)  61.2 us
    all_gather x1, blocking collectives, local(): lax.all_gather(cotangent, 'chan', axis=1, tiled=True)  29.6 us
    all_to_all x2, waiting for transfers between devices, copy_for_each(): lax.all_to_all(jnp.broadcast_to(value[None], (length, *value.shape)), axi...  17.1 us
    psum x1, blocking collectives, local(): square_total = lax.psum(jnp.sum(gated * gated, axis=1), 'chan')  16.8 us
    all_gather x2, waiting for transfers between devices, prefix_by_axis(): lax.all_gather(part.astype(kind), axis)  16.6 us
    all_to_all x2, starting transfers between devices, copy_for_each(): lax.all_to_all(jnp.broadcast_to(value[None], (length, *value.shape)), axi...  11.4 us
    all_to_all x1, starting transfers between devices, sent_and_summed(): lax.all_to_all(in_blocks(value, dim, length), axis, 0, 0, tiled=True)  7.55 us
  transfers between devices with their start and end apart: 5, of which 3 were waited for; matrix products, arithmetic and copies ran while one was open for 3% of the time, Pallas kernels for 0%

commit v1 on v0

--- a/solution.py
+++ b/solution.py
@@ -178,7 +178,7 @@
     ssd_out = ssd_out + skip_d[None, :, None] * x_heads.astype(jnp.float32)
     gate_act = jax.nn.silu(gate_z[0].astype(jnp.float32))
     gated = ssd_out.reshape(seq_len, local_width) * gate_act
-    square_total = lax.psum(jnp.sum(gated * gated, axis=1), "chan")
+    square_total = jnp.sum(lax.all_gather(jnp.sum(gated * gated, axis=1), "chan"), axis=0)
     inv_rms = lax.rsqrt(square_total / total_width + NORM_EPS)
     normed = (gated * norm_gain).astype(jnp.bfloat16)
     w_cols = w_out

time: 207 us -> 221 us (1.068)
  the two profiles are of different devices: /device:TPU:8 before, /device:TPU:16 now
where the time goes in v1:
time: 221 us; the launch traced here: 220 us
  blocking collectives  120 us (54%)
  waiting for transfers between devices  33.8 us (15%)
  starting transfers between devices  20.8 us (9%)
  between operations  15.3 us (7%)
  other arithmetic  13.9 us (6%)
  matrix products  9.75 us (4%)
  local copies, waits for them, and re-layouts  6.56 us (3%)
    all_gather x5, blocking collectives, prefix_by_axis(): lax.all_gather(part.astype(kind), axis)  60 us
    all_gather x1, blocking collectives, local(): lax.all_gather(cotangent, 'chan', axis=1, tiled=True)  29.8 us
    all_gather x2, waiting for transfers between devices, prefix_by_axis(): lax.all_gather(part.astype(kind), axis)  17.4 us
    all_to_all x2, waiting for transfers between devices, copy_for_each(): lax.all_to_all(jnp.broadcast_to(value[None], (length, *value.shape)), axi...  16.4 us
    all_gather x1, blocking collectives, local(): lax.all_gather(jnp.sum(gated * gated, axis=1), 'chan')  15.8 us
    psum x1, blocking collectives, local(): lax.psum(jnp.sum(cotangent.astype(jnp.float32) * projected, axis=1), 'chan')  14.6 us
    all_to_all x2, starting transfers between devices, copy_for_each(): lax.all_to_all(jnp.broadcast_to(value[None], (length, *value.shape)), axi...  13.4 us
    all_to_all x1, starting transfers between devices, sent_and_summed(): lax.all_to_all(in_blocks(value, dim, length), axis, 0, 0, tiled=True)  7.38 us
  transfers between devices with their start and end apart: 5, of which 3 were waited for; matrix products, arithmetic and copies ran while one was open for 3% of the time, Pallas kernels for 0%

profile of v1, /device:TPU:16, one launch (start us, length us, event | category | flops | bytes accessed | tf_op | source)
XLA Modules:
  0.0 220.3 jit_solution(4687219020408340689)
XLA Ops:
  7.3 1.0 reduce-window_clone.1
  8.3 0.7 subtract_bitcast_fusion
  8.9 0.1 compare_reduce_fusion
  9.0 0.1 copy.85
  9.1 0.2 broadcast_in_dim.163
  9.3 0.5 slice.212
  9.8 0.1 reduce.6
  10.6 0.8 copy.86
  11.4 0.2 reduce_window_sum.27
  11.6 0.7 broadcast_compare_fusion.1
  12.2 0.8 copy.89
  13.0 0.1 exponential_select_fusion
  13.2 0.1 copy.94
  13.4 0.9 fusion.16
  14.3 0.1 copy.95
  14.4 0.8 fusion.14
  15.3 16.3 %all-gather.4 = bf16[8,1,8]{2,1,0:T(2,128)(2,1)S(1)} all-gather(bf16[1,1,8]{2,1,0:T(2,128)(2,1)S(1)} %get-tuple-element.116), channel_id=1, replica_groups=mesh['seq_0'=4,'seq_1'=8,'chan'=8,'dp'=2] {'seq_1'}, dimensions={0}, use_global_device_ids=true | all-gather | bytes 144 | tf_op jit(solution)/shard_map/all_gather | solution.py:24
  31.6 0.5 convert_bitcast_fusion.2
  32.1 7.8 %all-gather.5 = bf16[4,1,8]{2,1,0:T(2,128)(2,1)S(1)} all-gather(bf16[1,1,8]{2,1,0:T(2,128)(2,1)S(1)} %get-tuple-element.121), channel_id=1, replica_groups=mesh['seq_0'=4,'seq_1'=8,'chan'=8,'dp'=2] {'seq_0'}, dimensions={0}, use_global_device_ids=true | all-gather | bytes 80 | tf_op jit(solution)/shard_map/all_gather | solution.py:24
  40.0 0.1 copy.91
  40.2 0.1 copy.96
  40.4 0.6 broadcast_select_fusion.7
  41.0 0.6 fusion.179
  41.6 0.1 fusion.147
  41.7 0.1 fusion.154
  41.8 0.2 fusion.9
  42.0 17.4 %all-gather.11.cloned.1.call-done = bf16[64,128,64]{1,2,0:T(8,128)(2,1)} async-done(((bf16[8,128,64]{1,2,0:T(8,128)(2,1)}), bf16[64,128,64]{1,2,0:T(8,128)(2,1)}) %all-gather.11.cloned.1.call-update) | async-done | bytes 1048592 | tf_op jit(solution)/shard_map/all_gather | solution.py:24
  59.4 1.6 fusion.79
  61.1 13.1 %all_gather.47 = bf16[4,8,128,64]{2,3,1,0:T(8,128)(2,1)S(1)} all-gather(bf16[1,8,128,64]{2,3,1,0:T(8,128)(2,1)S(1)} %fusion.79), channel_id=1, replica_groups=mesh['seq_0'=4,'seq_1'=8,'chan'=8,'dp'=2] {'seq_0'}, dimensions={0}, use_global_device_ids=true | all-gather | bytes 655360 | tf_op jit(solution)/shard_map/all_gather | solution.py:24
  74.2 1.9 fusion.8
  76.2 0.9 multiply_reduce_fusion.1
  77.1 0.1 copy.97
  77.3 0.5 convolution_convert_fusion
  77.8 0.8 copy.110
  78.6 7.4 %all-to-all-start = ((bf16[8,256,128]{1,2,0:T(8,128)(2,1)}), bf16[8,256,128]{1,2,0:T(8,128)(2,1)S(1)}, u32[]{:S(2)}, u32[]{:S(2)}) async-start(bf16[8,256,128]{1,2,0:T(8,128)(2,1)} %bitcast.431), calls=%async_computation | async-start | bytes 1048576 | tf_op jit(solution)/shard_map/all_to_all | solution.py:47
  86.1 0.1 copy.100
  86.2 29.8 %all-gather.2 = bf16[1,128,2048]{2,1,0:T(8,128)(2,1)S(1)} all-gather(bf16[1,128,256]{2,1,0:T(8,128)(2,1)} %param.20), channel_id=4, replica_groups=mesh['seq_0'=4,'seq_1'=8,'chan'=8,'dp'=2] {'chan'}, dimensions={2}, use_global_device_ids=true | all-gather | bytes 589824 | tf_op jit(solution)/shard_map/all_gather | solution.py:196
  116.0 15.8 %all-gather.6 = f32[8,1,128]{2,1,0:T(1,128)S(1)} all-gather(f32[1,1,128]{2,1,0:T(1,128)} %bitcast.446), channel_id=3, replica_groups=mesh['seq_0'=4,'seq_1'=8,'chan'=8,'dp'=2] {'chan'}, dimensions={0}, use_global_device_ids=true | all-gather | bytes 4608 | tf_op jit(solution)/shard_map/all_gather | solution.py:181
  131.8 0.5 reduce_sum.80
  132.3 0.7 add_rsqrt_fusion
  133.1 1.6 fusion.88
  134.7 14.6 %psum.7 = f32[128]{0:T(128)S(1)} all-reduce(f32[128]{0:T(128)S(1)} %get-tuple-element.98), channel_id=1, replica_groups=mesh['seq_0'=4,'seq_1'=8,'chan'=8,'dp'=2] {'chan'}, use_global_device_ids=true, to_apply=%region_8.9 | all-reduce | flops 128 | bytes 1024 | tf_op jit(solution)/shard_map/psum | solution.py:201
  149.2 0.7 fusion.178
  149.9 1.9 fusion.18
  152.0 0.1 copy.101
  152.1 0.8 fusion.13
  153.0 9.4 %all-gather.7 = bf16[4,1,8]{2,1,0:T(2,128)(2,1)S(1)} all-gather(bf16[1,1,8]{2,1,0:T(2,128)(2,1)S(1)} %copy-done.28), channel_id=1, replica_groups=mesh['seq_0'=4,'seq_1'=8,'chan'=8,'dp'=2] {'seq_0'}, dimensions={0}, use_global_device_ids=true | all-gather | bytes 80 | tf_op jit(solution)/shard_map/all_gather | solution.py:24
  162.3 0.1 reduce_sum.86
  162.4 0.1 reduce_sum.87
  162.5 0.6 broadcast_in_dim.174
  163.1 7.1 %all-to-all-start.2 = ((f32[64,1,8]{2,1,0:T(1,128)}), f32[64,1,8]{2,1,0:T(1,128)S(1)}, u32[]{:S(2)}, u32[]{:S(2)}) async-start(f32[64,1,8]{2,1,0:T(1,128)} %broadcast_in_dim.174), calls=%async_computation.2 | async-start | bytes 65536 | tf_op jit(solution)/shard_map/all_to_all | solution.py:53
  170.2 7.8 %all-to-all-done.2 = f32[64,1,8]{2,1,0:T(1,128)S(1)} async-done(((f32[64,1,8]{2,1,0:T(1,128)}), f32[64,1,8]{2,1,0:T(1,128)S(1)}, u32[]{:S(2)}, u32[]{:S(2)}) %all-to-all-start.2) | async-done | bytes 2080 | tf_op jit(solution)/shard_map/all_to_all | solution.py:53
  178.1 0.7 broadcast_in_dim.173
  178.8 6.3 %all-to-all-start.1 = ((f32[64,1,512]{2,1,0:T(1,128)}), f32[64,1,512]{2,1,0:T(1,128)S(1)}, u32[]{:S(2)}, u32[]{:S(2)}) async-start(f32[64,1,512]{2,1,0:T(1,128)} %broadcast_in_dim.173), calls=%async_computation.1 | async-start | bytes 262144 | tf_op jit(solution)/shard_map/all_to_all | solution.py:53
  185.1 0.2 fusion.7
  185.3 0.1 copy.99
  185.4 0.6 reduce_sum.88
  186.0 8.5 %all-to-all-done.1 = f32[64,1,512]{2,1,0:T(1,128)S(1)} async-done(((f32[64,1,512]{2,1,0:T(1,128)}), f32[64,1,512]{2,1,0:T(1,128)S(1)}, u32[]{:S(2)}, u32[]{:S(2)}) %all-to-all-start.1) | async-done | bytes 131104 | tf_op jit(solution)/shard_map/all_to_all | solution.py:53
  194.6 0.7 reduce_sum.84
  195.3 1.6 fusion.62
  197.0 13.4 %all_gather.54 = bf16[4,8,128,64]{2,3,1,0:T(8,128)(2,1)S(1)} all-gather(bf16[1,8,128,64]{2,3,1,0:T(8,128)(2,1)S(1)} %fusion.62), channel_id=1, replica_groups=mesh['seq_0'=4,'seq_1'=8,'chan'=8,'dp'=2] {'seq_0'}, dimensions={0}, use_global_device_ids=true | all-gather | bytes 655360 | tf_op jit(solution)/shard_map/all_gather | solution.py:24
  210.4 1.9 fusion.6
  212.4 0.4 fusion.12
  212.7 0.8 copy.104
  (88 shorter events, 0.6 us)
Async XLA Ops:
  7.2 70.1 %copy-start = (bf16[512,2048]{1,0:T(8,128)(2,1)S(1)}, bf16[512,2048]{1,0:T(8,128)(2,1)}, u32[]{:S(2)}) copy-start(bf16[512,2048]{1,0:T(8,128)(2,1)} %param.19) | copy-start | bytes 6291460
  7.2 32.8 %copy-start.1 = (bf16[1,128,512]{2,1,0:T(8,128)(2,1)S(1)}, bf16[1,128,512]{2,1,0:T(8,128)(2,1)}, u32[]{:S(2)}) copy-start(bf16[1,128,512]{2,1,0:T(8,128)(2,1)} %param.11) | copy-start | bytes 393220
  7.2 7.2 %copy-start.4 = (bf16[1,128,128]{2,1,0:T(8,128)(2,1)S(1)}, bf16[1,128,128]{2,1,0:T(8,128)(2,1)}, u32[]{:S(2)}) copy-start(bf16[1,128,128]{2,1,0:T(8,128)(2,1)} %param.13) | copy-start | bytes 98308
  7.2 33.0 %copy-start.7 = (bf16[1,128,512]{2,1,0:T(8,128)(2,1)S(1)}, bf16[1,128,512]{2,1,0:T(8,128)(2,1)}, u32[]{:S(2)}) copy-start(bf16[1,128,512]{2,1,0:T(8,128)(2,1)} %param.12) | copy-start | bytes 393220
  7.2 34.4 %copy-start.2 = (bf16[1,128,128]{2,1,0:T(8,128)(2,1)S(1)}, bf16[1,128,128]{2,1,0:T(8,128)(2,1)}, u32[]{:S(2)}) copy-start(bf16[1,128,128]{2,1,0:T(8,128)(2,1)} %param.14) | copy-start | bytes 98308
  7.2 52.2 %all-gather.11.cloned.1.call-start = ((), (), s32[]{:S(2)}) async-start(), calls=%async_computation.3 | async-start | bytes 1179648 | tf_op jit(solution)/shard_map/all_gather | solution.py:24
  11.6 3.7 %copy-start.24 = (f32[8]{0:T(128)}, f32[8]{0:T(128)S(1)}, u32[]{:S(2)}) copy-start(f32[8]{0:T(128)S(1)} %fusion.160) | copy-start | bytes 100
  40.2 36.0 %copy-start.22 = (f32[8,128]{1,0:T(8,128)}, f32[8,128]{1,0:T(8,128)S(1)}, u32[]{:S(2)}) copy-start(f32[8,128]{1,0:T(8,128)S(1)} %copy.87) | copy-start | bytes 12292
  41.5 34.6 %copy-start.12 = (f32[8]{0:T(128)}, f32[8]{0:T(128)S(1)}, u32[]{:S(2)}) copy-start(f32[8]{0:T(128)S(1)} %get-tuple-element.125) | copy-start | bytes 100
  41.5 34.6 %copy-start.14 = (f32[8]{0:T(128)}, f32[8]{0:T(128)S(1)}, u32[]{:S(2)}) copy-start(f32[8]{0:T(128)S(1)} %get-tuple-element.126) | copy-start | bytes 100
  41.5 34.6 %copy-start.16 = (f32[8]{0:T(128)}, f32[8]{0:T(128)S(1)}, u32[]{:S(2)}) copy-start(f32[8]{0:T(128)S(1)} %get-tuple-element.127) | copy-start | bytes 100
  41.5 34.6 %copy-start.18 = (f32[8]{0:T(128)}, f32[8]{0:T(128)S(1)}, u32[]{:S(2)}) copy-start(f32[8]{0:T(128)S(1)} %get-tuple-element.128) | copy-start | bytes 100
  41.7 34.5 %copy-start.10 = (pred[128,128]{1,0:T(8,128)(4,1)}, pred[128,128]{1,0:T(8,128)(4,1)S(1)}, u32[]{:S(2)}) copy-start(pred[128,128]{1,0:T(8,128)(4,1)S(1)} %fusion.147) | copy-start | bytes 49156
  41.8 34.4 %copy-start.8 = (f32[128,128]{1,0:T(8,128)}, f32[128,128]{1,0:T(8,128)S(1)}, u32[]{:S(2)}) copy-start(f32[128,128]{1,0:T(8,128)S(1)} %fusion.154) | copy-start | bytes 196612
  74.2 2.0 copy-start.20
  74.2 2.0 copy-start.31
  76.2 1.1 copy-start.30
  77.3 1.3 copy-start.6
  78.6 54.4 %all-to-all-start = ((bf16[8,256,128]{1,2,0:T(8,128)(2,1)}), bf16[8,256,128]{1,2,0:T(8,128)(2,1)S(1)}, u32[]{:S(2)}, u32[]{:S(2)}) async-start(bf16[8,256,128]{1,2,0:T(8,128)(2,1)} %bitcast.431), calls=%async_computation | async-start | bytes 1048576 | tf_op jit(solution)/shard_map/all_to_all | solution.py:47
  86.0 109.3 %all-gather.13.cloned.1.call-start = ((), (), s32[]{:S(2)}) async-start(), calls=%async_computation.4 | async-start | bytes 1179648 | tf_op jit(solution)/shard_map/all_gather | solution.py:24
  149.9 2.2 %copy-start.3 = (bf16[1,128,128]{2,1,0:T(8,128)(2,1)S(1)}, bf16[1,128,128]{2,1,0:T(8,128)(2,1)}, u32[]{:S(2)}) copy-start(bf16[1,128,128]{2,1,0:T(8,128)(2,1)} %param.14) | copy-start | bytes 98308
  149.9 2.2 %copy-start.25 = (f32[8]{0:T(128)S(1)}, f32[8]{0:T(128)}, u32[]{:S(2)}) copy-start(f32[8]{0:T(128)} %copy-done.24) | copy-start | bytes 100
  149.9 3.1 %copy-start.28 = (bf16[1,1,8]{2,1,0:T(2,128)(2,1)S(1)}, bf16[1,1,8]{2,1,0:T(2,128)(2,1)}, u32[]{:S(2)}) copy-start(bf16[1,1,8]{2,1,0:T(2,128)(2,1)} %get-tuple-element.120) | copy-start | bytes 52
  149.9 35.2 %copy-start.5 = (bf16[1,128,128]{2,1,0:T(8,128)(2,1)S(1)}, bf16[1,128,128]{2,1,0:T(8,128)(2,1)}, u32[]{:S(2)}) copy-start(bf16[1,128,128]{2,1,0:T(8,128)(2,1)} %param.13) | copy-start | bytes 98308
  151.9 43.4 %copy-start.13 = (f32[8]{0:T(128)S(1)}, f32[8]{0:T(128)}, u32[]{:S(2)}) copy-start(f32[8]{0:T(128)} %copy-done.12) | copy-start | bytes 100
  151.9 43.4 %copy-start.15 = (f32[8]{0:T(128)S(1)}, f32[8]{0:T(128)}, u32[]{:S(2)}) copy-start(f32[8]{0:T(128)} %copy-done.14) | copy-start | bytes 100
  151.9 43.4 %copy-start.17 = (f32[8]{0:T(128)S(1)}, f32[8]{0:T(128)}, u32[]{:S(2)}) copy-start(f32[8]{0:T(128)} %copy-done.16) | copy-start | bytes 100
  151.9 43.4 %copy-start.19 = (f32[8]{0:T(128)S(1)}, f32[8]{0:T(128)}, u32[]{:S(2)}) copy-start(f32[8]{0:T(128)} %copy-done.18) | copy-start | bytes 100
  151.9 43.4 %copy-start.26 = (f32[8]{0:T(128)S(1)}, f32[8]{0:T(128)}, u32[]{:S(2)}) copy-start(f32[8]{0:T(128)} %get-tuple-element.119) | copy-start | bytes 100
  151.9 43.4 %copy-start.27 = (f32[8]{0:T(128)S(1)}, f32[8]{0:T(128)}, u32[]{:S(2)}) copy-start(f32[8]{0:T(128)} %get-tuple-element.122) | copy-start | bytes 100
  151.9 58.4 %copy-start.29 = (f32[8]{0:T(128)S(1)}, f32[8]{0:T(128)}, u32[]{:S(2)}) copy-start(f32[8]{0:T(128)} %get-tuple-element.117) | copy-start | bytes 100
  163.1 14.9 %all-to-all-start.2 = ((f32[64,1,8]{2,1,0:T(1,128)}), f32[64,1,8]{2,1,0:T(1,128)S(1)}, u32[]{:S(2)}, u32[]{:S(2)}) async-start(f32[64,1,8]{2,1,0:T(1,128)} %broadcast_in_dim.174), calls=%async_computation.2 | async-start | bytes 65536 | tf_op jit(solution)/shard_map/all_to_all | solution.py:53
  178.8 15.8 %all-to-all-start.1 = ((f32[64,1,512]{2,1,0:T(1,128)}), f32[64,1,512]{2,1,0:T(1,128)S(1)}, u32[]{:S(2)}, u32[]{:S(2)}) async-start(f32[64,1,512]{2,1,0:T(1,128)} %broadcast_in_dim.173), calls=%async_computation.1 | async-start | bytes 262144 | tf_op jit(solution)/shard_map/all_to_all | solution.py:53
  210.3 2.0 copy-start.9
  210.3 2.0 copy-start.11
  210.3 2.0 copy-start.21
  210.3 2.0 copy-start.23
  210.3 2.0 copy-start.32
Sparse Core Ops, SparseCore 0:
  15.4 43.9 all-gather.10
  153.1 38.1 all-gather.12
